TPU v7x, 32 devices: a whole 2x2x4 slice. The times are simulated.
32 devices in a mesh: dom: 8 (over z, y), orb: 4 (over x, core).
Axes of the slice: x: 2, y: 2, z: 4, core: 2. Of those that a mesh axis runs over, the one named last changes fastest.
Arguments:
- orbitals: bfloat16 [16, 4, 1024, 512], P('dom', None, None, 'orb'), may hold values from -6 to 6
- slot_ids: int32 [16, 4], P('dom'), may hold values from 0 to 15, as said below
- slot_count: int32 [16], P('dom'), may hold values from 1 to 4, as said below
- band_tiles: bfloat16 [16, 3, 512, 512], P(None, None, 'dom', 'orb'), may hold values from -0.15625 to 0.15625
- pattern: int32 [16, 3], replicated, may hold values 0 or 1
- occupation: float32 [16, 512], P(None, 'orb'), may hold values from 0.0005 to 0.005
Outputs:
- rotated: bfloat16 [16, 4, 1024, 512], P('dom', None, None, 'orb')
- density: float32 [16, 1024], P('dom')
Inputs may be any that keep to these rules, and one draw needn't show every extreme that they name: `slot_ids`: each row names 4 consecutive orbital blocks counted modulo 16: slot l holds (s + l) mod 16, where the first block s of a grid block may be any of the 16 blocks. The slots in use on grid block g are its first slot_count[g]; some grid block uses all 4.
All inputs are finite; a program needn't handle non-finite values.
Results may differ from a plain program's by a relative error of at most 0.00094.
Values may be sent and summed in bfloat16 or wider, within the bound.
A program may use at most 128 MiB of HBM per device.

v0:
```python
import jax
import jax.numpy as jnp
from jax import lax
from jax.sharding import PartitionSpec as P


def select_tiles(band_full, pattern, slot_ids, slot_count):
    slots_per = slot_ids.shape[1]
    band_count = pattern.shape[1]
    half_band = (band_count - 1) // 2
    active = jnp.arange(slots_per, dtype=jnp.int32)[None, :] < slot_count[:, None]
    source = slot_ids[:, :, None]
    target = slot_ids[:, None, :]
    offset = target - source + half_band
    inside = (offset >= 0) & (offset < band_count)
    column = jnp.clip(offset, 0, band_count - 1)
    keeping = inside & (pattern[source, column] == 1) & active[:, :, None] & active[:, None, :]
    picked = band_full[source, column]
    return jnp.where(keeping[:, :, :, None, None], picked, jnp.zeros((), picked.dtype))


def rotate(values, tile_set):
    return jnp.einsum("glpi,glmij->gmpj", values, tile_set, preferred_element_type=jnp.float32)


def local(orbitals, slot_ids, slot_count, band_tiles, pattern, occupation):
    all_rows = lax.all_gather(band_tiles, "dom", axis=2, tiled=True)
    tile_set = select_tiles(all_rows, pattern, slot_ids, slot_count)
    rotated_f = rotate(lax.all_gather(orbitals, "orb", axis=3, tiled=True), tile_set)
    rotated = rotated_f.astype(jnp.bfloat16)
    onehot = (
        slot_ids[:, :, None] == jnp.arange(occupation.shape[0], dtype=jnp.int32)[None, None, :]
    ).astype(jnp.float32)
    weights = jnp.einsum("glb,bj->glj", onehot, occupation, precision=lax.Precision.HIGHEST)
    widened = rotated.astype(jnp.float32)
    square = widened * widened
    partial_density = jnp.einsum("gmpj,gmj->gp", square, weights, precision=lax.Precision.HIGHEST)
    density = lax.psum(partial_density, "orb")
    return (rotated, density)


def solution(mesh):
    placed = (
        P("dom", None, None, "orb"),
        P("dom", None),
        P("dom"),
        P(None, None, "dom", "orb"),
        P(),
        P(None, "orb"),
    )
    return jax.shard_map(
        local,
        mesh=mesh,
        in_specs=placed,
        out_specs=(P("dom", None, None, "orb"), P("dom", None)),
        check_vma=False,
    )
```

profile of v0, /device:TPU:0, one launch (start us, length us, event | category | flops | bytes accessed | tf_op | source)
XLA Modules:
  0.0 198.5 jit_solution(10908176028303874434)
XLA Ops:
  7.2 0.0 copy-start
  7.2 0.0 copy-start.2
  7.2 0.0 copy-start.1
  7.2 0.0 copy-start.3
  7.2 0.0 all-gather.3.cloned.1.call-start
  7.3 0.7 all-gather.3.cloned.1.call-update
  7.9 0.0 all-gather.5.cloned.1.call-start
  8.0 0.7 all-gather.5.cloned.1.call-update
  8.7 0.7 fusion.26
  9.4 0.8 fusion.17
  10.2 0.1 reshape.76
  10.3 0.0 copy-done.1
  10.3 0.8 gather_fusion
  11.1 0.1 reshape.89
  11.2 0.0 copy-done.3
  11.2 0.1 iota_compare_fusion.2
  11.2 0.0 copy-done.2
  11.2 0.1 fusion.23
  11.3 0.1 copy.11
  11.4 0.0 copy-done
  11.4 0.2 fusion.13
  11.7 100.0 %all-gather.3.cloned.1.call-done = bf16[16,3,512,128]{3,2,1,0:T(8,128)(2,1)} async-done(((bf16[16,3,64,128]{3,2,1,0:T(8,128)(2,1)}), bf16[16,3,512,128]{3,2,1,0:T(8,128)(2,1)}) %all-gather.3.cloned.1.call-update) | async-done | bytes 6291472 | tf_op jit(solution)/shard_map/all_gather | solution.py:27
  111.7 5.8 %gather_fusion.1 = bf16[32,512,128]{2,1,0:T(8,128)(2,1)} fusion(bf16[16,3,512,128]{3,2,1,0:T(8,128)(2,1)} %all-gather.3.cloned.1.call-done, s32[32]{0:T(128)S(1)} %reshape.76), kind=kCustom, calls=%fused_computation.1 | custom fusion | bytes 8388864 | tf_op jit(solution)/shard_map/gather | solution.py:18
  117.5 7.6 %copy.12 = bf16[2,4,4,512,128]{3,4,1,2,0:T(8,128)(2,1)} copy(bf16[2,4,4,512,128]{4,3,2,1,0:T(8,128)(2,1)} %bitcast.27) | data formatting | bytes 8388608 | tf_op jit(solution)/shard_map/gather | solution.py:18
  125.1 45.7 %all-gather.5.cloned.1.call-done = bf16[2,4,1024,512]{3,2,1,0:T(8,128)(2,1)} async-done(((bf16[2,4,1024,128]{3,2,1,0:T(8,128)(2,1)}), bf16[2,4,1024,512]{3,2,1,0:T(8,128)(2,1)}) %all-gather.5.cloned.1.call-update) | async-done | bytes 8388624 | tf_op jit(solution)/shard_map/all_gather | solution.py:29
  170.8 9.2 %fusion.7 = bf16[2,4,1024,128]{2,3,1,0:T(8,128)(2,1)S(1)} fusion(bf16[2,4,1024,512]{3,2,1,0:T(8,128)(2,1)} %all-gather.5.cloned.1.call-done, bf16[2,4,4,512,128]{3,4,1,2,0:T(8,128)(2,1)} %copy.12, pred[2,4,4]{1,2,0:T(4,128)(4,1)S(1)} %copy.11), kind=kOutput, calls=%fused_computation.10 | convolution fusion | flops 4298113024 | bytes 14680096 | tf_op jit(solution)/shard_map/glpi,glmij->gmpj/dot_general | solution.py:23
  180.0 2.6 %copy.13 = bf16[2,4,1024,128]{3,2,1,0:T(8,128)(2,1)} copy(bf16[2,4,1024,128]{2,3,1,0:T(8,128)(2,1)S(1)} %fusion.7) | data formatting | bytes 4194304
  182.6 2.5 %fusion.2 = f32[2,1,1024,1]{2,1,3,0:T(1,128)S(1)} fusion(f32[2,4,128,1]{2,3,1,0:T(1,128)S(1)} %bitcast.29, bf16[2,4,1024,128]{2,3,1,0:T(8,128)(2,1)S(1)} %fusion.7), kind=kOutput, calls=%fused_computation.5 | convolution fusion | flops 14680064 | bytes 2109440 | tf_op jit(solution)/shard_map/gmpj,gmj->gp/dot_general | solution.py:37
  185.1 6.6 %psum.7 = f32[2,1024]{1,0:T(2,128)} all-reduce(f32[2,1024]{1,0:T(2,128)S(1)} %bitcast.28), channel_id=1, replica_groups=mesh['dom'=8,'orb'=4] {'orb'}, use_global_device_ids=true, to_apply=%region_0.1 | all-reduce | flops 2048 | bytes 16384 | tf_op jit(solution)/shard_map/psum | solution.py:38
  (2 shorter events, 0.0 us)
Async XLA Ops:
  7.2 4.3 %copy-start = (f32[16,128]{1,0:T(8,128)S(1)}, f32[16,128]{1,0:T(8,128)}, u32[]{:S(2)}) copy-start(f32[16,128]{1,0:T(8,128)} %param.11) | copy-start | bytes 24580
  7.2 4.1 %copy-start.2 = (s32[2,4]{1,0:T(2,128)S(1)}, s32[2,4]{1,0:T(2,128)}, u32[]{:S(2)}) copy-start(s32[2,4]{1,0:T(2,128)} %param.7) | copy-start | bytes 100
  7.2 3.1 %copy-start.1 = (s32[16,3]{0,1:T(4,128)S(1)}, s32[16,3]{0,1:T(4,128)}, u32[]{:S(2)}) copy-start(s32[16,3]{0,1:T(4,128)} %param.10) | copy-start | bytes 580
  7.2 4.0 %copy-start.3 = (s32[2]{0:T(128)S(1)}, s32[2]{0:T(128)}, u32[]{:S(2)}) copy-start(s32[2]{0:T(128)} %param.8) | copy-start | bytes 28
  7.2 104.4 %all-gather.3.cloned.1.call-start = ((), (), s32[]{:S(2)}) async-start(), calls=%async_computation | async-start | bytes 7077888 | tf_op jit(solution)/shard_map/all_gather | solution.py:27
  7.9 162.9 %all-gather.5.cloned.1.call-start = ((), (), s32[]{:S(2)}) async-start(), calls=%async_computation.1 | async-start | bytes 10485760 | tf_op jit(solution)/shard_map/all_gather | solution.py:29
Sparse Core Ops, SparseCore 0:
  10.2 101.4 all-gather.2
  113.2 57.5 all-gather.4
where the time goes:
time: 199 us; the launch traced here: 198 us
  waiting for transfers between devices  147 us (74%)
  local copies, waits for them, and re-layouts  17.1 us (9%)
  between operations  14.1 us (7%)
  matrix products  11.9 us (6%)
  blocking collectives  6.59 us (3%)
    all_gather x1, waiting for transfers between devices, local(): all_rows = lax.all_gather(band_tiles, 'dom', axis=2, tiled=True)  100 us
    all_gather x1, waiting for transfers between devices, local(): lax.all_gather(orbitals, 'orb', axis=3, tiled=True)  45.7 us
    gather x2, local copies, waits for them, and re-layouts, select_tiles(): picked = band_full[source, column]  13.4 us
    dot_general x1, matrix products, rotate(): jnp.einsum('glpi,glmij->gmpj', values, tile_set, preferred_element_type=j...  9.19 us
    psum x1, blocking collectives, local(): density = lax.psum(partial_density, 'orb')  6.59 us
  transfers between devices with their start and end apart: 2, of which 2 were waited for; matrix products, arithmetic and copies ran while one was open for 8% of the time, Pallas kernels for 0%

commit v1 on v0

--- a/solution.py
+++ b/solution.py
@@ -2,6 +2,11 @@
 import jax.numpy as jnp
 from jax import lax
 from jax.sharding import PartitionSpec as P
+
+
+def stack_and_merge(x, axis, dim):
+    shards = lax.all_gather(x, axis)
+    return jnp.concatenate(shards, axis=dim)
 
 
 def select_tiles(band_full, pattern, slot_ids, slot_count):
@@ -26,7 +31,7 @@
 def local(orbitals, slot_ids, slot_count, band_tiles, pattern, occupation):
     all_rows = lax.all_gather(band_tiles, "dom", axis=2, tiled=True)
     tile_set = select_tiles(all_rows, pattern, slot_ids, slot_count)
-    rotated_f = rotate(lax.all_gather(orbitals, "orb", axis=3, tiled=True), tile_set)
+    rotated_f = rotate(stack_and_merge(orbitals, "orb", 3), tile_set)
     rotated = rotated_f.astype(jnp.bfloat16)
     onehot = (
         slot_ids[:, :, None] == jnp.arange(occupation.shape[0], dtype=jnp.int32)[None, None, :]

time: 199 us -> 223 us (1.12)
  local copies, waits for them, and re-layouts: 17.1 us -> 42.4 us
    reshape x0 -> x1, local copies, waits for them, and re-layouts: none -> 13.1 us  [stack_and_merge(): return jnp.concatenate(shards, axis=dim)]
    all_gather x0 -> x1, local copies, waits for them, and re-layouts: none -> 12.2 us  [stack_and_merge(): shards = lax.all_gather(x, axis)]
  transfers between devices with their start and end apart: 2 -> 2, of which waited for: 2 -> 2; matrix products, arithmetic and copies ran while one was open for 8% -> 7% of each run, Pallas kernels for 0% -> 0%
where the time goes in v1:
time: 223 us
  waiting for transfers between devices  146 us (65%)
  local copies, waits for them, and re-layouts  42.4 us (19%)
  between operations  14.1 us (6%)
  matrix products  11.9 us (5%)
  blocking collectives  6.59 us (3%)
    all_gather x1, waiting for transfers between devices, local(): all_rows = lax.all_gather(band_tiles, 'dom', axis=2, tiled=True)  100 us
    all_gather x1, waiting for transfers between devices, stack_and_merge(): shards = lax.all_gather(x, axis)  44.6 us
    gather x2, local copies, waits for them, and re-layouts, select_tiles(): picked = band_full[source, column]  13.4 us
    reshape x1, local copies, waits for them, and re-layouts, stack_and_merge(): return jnp.concatenate(shards, axis=dim)  13.1 us
    all_gather x1, local copies, waits for them, and re-layouts, stack_and_merge(): shards = lax.all_gather(x, axis)  12.2 us
    dot_general x1, matrix products, rotate(): jnp.einsum('glpi,glmij->gmpj', values, tile_set, preferred_element_type=j...  9.19 us
    psum x1, blocking collectives, local(): density = lax.psum(partial_density, 'orb')  6.59 us
  transfers between devices with their start and end apart: 2, of which 2 were waited for; matrix products, arithmetic and copies ran while one was open for 7% of the time, Pallas kernels for 0%

profile of v1, /device:TPU:0, one launch (start us, length us, event | category | flops | bytes accessed | tf_op | source)
XLA Modules:
  0.0 222.7 jit_solution(8748058482375309335)
XLA Ops:
  7.2 0.0 copy-start
  7.2 0.0 copy-start.2
  7.2 0.0 copy-start.1
  7.2 0.0 copy-start.3
  7.2 0.0 all-gather.4.cloned.1.call-start
  7.3 0.7 all-gather.4.cloned.1.call-update
  7.9 0.0 all-gather.6.cloned.1.call-start
  8.0 0.7 all-gather.6.cloned.1.call-update
  8.7 0.7 fusion.26
  9.4 0.8 fusion.17
  10.2 0.1 reshape.84
  10.3 0.0 copy-done.1
  10.3 0.8 gather_fusion
  11.1 0.1 reshape.98
  11.2 0.0 copy-done.3
  11.2 0.1 iota_compare_fusion.2
  11.2 0.0 copy-done.2
  11.2 0.1 fusion.23
  11.3 0.1 copy.16
  11.4 0.0 copy-done
  11.4 0.2 fusion.13
  11.7 100.0 %all-gather.4.cloned.1.call-done = bf16[16,3,512,128]{3,2,1,0:T(8,128)(2,1)} async-done(((bf16[16,3,64,128]{3,2,1,0:T(8,128)(2,1)}), bf16[16,3,512,128]{3,2,1,0:T(8,128)(2,1)}) %all-gather.4.cloned.1.call-update) | async-done | bytes 6291472 | tf_op jit(solution)/shard_map/all_gather | solution.py:32
  111.7 5.8 %gather_fusion.1 = bf16[32,512,128]{2,1,0:T(8,128)(2,1)} fusion(bf16[16,3,512,128]{3,2,1,0:T(8,128)(2,1)} %all-gather.4.cloned.1.call-done, s32[32]{0:T(128)S(1)} %reshape.84), kind=kCustom, calls=%fused_computation.1 | custom fusion | bytes 8388864 | tf_op jit(solution)/shard_map/gather | solution.py:23
  117.5 7.6 %copy.17 = bf16[2,4,4,512,128]{3,4,1,2,0:T(8,128)(2,1)} copy(bf16[2,4,4,512,128]{4,3,2,1,0:T(8,128)(2,1)} %bitcast.30) | data formatting | bytes 8388608 | tf_op jit(solution)/shard_map/gather | solution.py:23
  125.1 44.6 %all-gather.6.cloned.1.call-done = bf16[8,4,1024,128]{3,2,1,0:T(8,128)(2,1)} async-done(((bf16[2,4,1024,128]{3,2,1,0:T(8,128)(2,1)}), bf16[8,4,1024,128]{3,2,1,0:T(8,128)(2,1)}) %all-gather.6.cloned.1.call-update) | async-done | bytes 8388624 | tf_op jit(solution)/shard_map/all_gather | solution.py:8
  169.7 12.2 %copy.26 = bf16[4,2,4,1024,128]{4,0,3,2,1:T(4,128)(2,1)} copy(bf16[4,2,4,1024,128]{4,3,2,1,0:T(8,128)(2,1)} %bitcast.31) | data formatting | bytes 16777216 | tf_op jit(solution)/shard_map/all_gather | solution.py:8
  181.9 13.1 %reshape.99 = bf16[2,4,1024,512,1]{3,2,1,0,4:T(8,128)(2,1)} reshape(bf16[2,4,1024,4,128]{4,3,2,1,0:T(4,128)(2,1)} %bitcast.29) | data formatting | bytes 16777216 | tf_op jit(solution)/shard_map/reshape | solution.py:9
  195.0 9.2 %fusion.7 = bf16[2,4,1024,128]{2,3,1,0:T(8,128)(2,1)S(1)} fusion(bf16[2,4,1024,512,1]{3,2,1,0,4:T(8,128)(2,1)} %reshape.99, bf16[2,4,4,512,128]{3,4,1,2,0:T(8,128)(2,1)} %copy.17, pred[2,4,4]{1,2,0:T(4,128)(4,1)S(1)} %copy.16), kind=kOutput, calls=%fused_computation.11 | convolution fusion | flops 4298113024 | bytes 14680096 | tf_op jit(solution)/shard_map/glpi,glmij->gmpj/dot_general | solution.py:28
  204.2 2.6 %copy.19 = bf16[2,4,1024,128]{3,2,1,0:T(8,128)(2,1)} copy(bf16[2,4,1024,128]{2,3,1,0:T(8,128)(2,1)S(1)} %fusion.7) | data formatting | bytes 4194304
  206.7 2.5 %fusion.2 = f32[2,1,1024,1]{2,1,3,0:T(1,128)S(1)} fusion(f32[2,4,128,1]{2,3,1,0:T(1,128)S(1)} %bitcast.33, bf16[2,4,1024,128]{2,3,1,0:T(8,128)(2,1)S(1)} %fusion.7), kind=kOutput, calls=%fused_computation.6 | convolution fusion | flops 14680064 | bytes 2109440 | tf_op jit(solution)/shard_map/gmpj,gmj->gp/dot_general | solution.py:42
  209.2 6.6 %psum.7 = f32[2,1024]{1,0:T(2,128)} all-reduce(f32[2,1024]{1,0:T(2,128)S(1)} %bitcast.32), channel_id=1, replica_groups=mesh['dom'=8,'orb'=4] {'orb'}, use_global_device_ids=true, to_apply=%region_0.1 | all-reduce | flops 2048 | bytes 16384 | tf_op jit(solution)/shard_map/psum | solution.py:43
  (2 shorter events, 0.0 us)
Async XLA Ops:
  7.2 4.3 %copy-start = (f32[16,128]{1,0:T(8,128)S(1)}, f32[16,128]{1,0:T(8,128)}, u32[]{:S(2)}) copy-start(f32[16,128]{1,0:T(8,128)} %param.11) | copy-start | bytes 24580
  7.2 4.1 %copy-start.2 = (s32[2,4]{1,0:T(2,128)S(1)}, s32[2,4]{1,0:T(2,128)}, u32[]{:S(2)}) copy-start(s32[2,4]{1,0:T(2,128)} %param.7) | copy-start | bytes 100
  7.2 3.1 %copy-start.1 = (s32[16,3]{0,1:T(4,128)S(1)}, s32[16,3]{0,1:T(4,128)}, u32[]{:S(2)}) copy-start(s32[16,3]{0,1:T(4,128)} %param.10) | copy-start | bytes 580
  7.2 4.0 %copy-start.3 = (s32[2]{0:T(128)S(1)}, s32[2]{0:T(128)}, u32[]{:S(2)}) copy-start(s32[2]{0:T(128)} %param.8) | copy-start | bytes 28
  7.2 104.4 %all-gather.4.cloned.1.call-start = ((), (), s32[]{:S(2)}) async-start(), calls=%async_computation | async-start | bytes 7077888 | tf_op jit(solution)/shard_map/all_gather | solution.py:32
  7.9 161.7 %all-gather.6.cloned.1.call-start = ((), (), s32[]{:S(2)}) async-start(), calls=%async_computation.1 | async-start | bytes 10485760 | tf_op jit(solution)/shard_map/all_gather | solution.py:8
Sparse Core Ops, SparseCore 0:
  10.2 101.4 all-gather.3
  113.2 56.4 all-gather.5
